TPU v7x, 512 devices: a whole 4x8x8 slice. The times are simulated.
512 devices in a mesh: lat: 128 (over z, y, core), chan: 4 (over x).
Axes of the slice: x: 4, y: 8, z: 8, core: 2. Of those that a mesh axis runs over, the one named last changes fastest.
Arguments:
- grid_in: bfloat16 [256, 384, 1024], P('chan', 'lat'), may hold values from -6 to 6
- quad_weights: float32 [384], P('lat'), may hold values from 0.5 to 2
- legendre: bfloat16 [384, 384, 384], P('lat'), as said below
- mixing: bfloat16 [2, 384, 256, 256], P(None, 'lat', 'chan'), may hold values from -0.375 to 0.375
Outputs:
- grid_out: bfloat16 [256, 384, 1024], P('chan', 'lat')
Inputs may be any that keep to these rules, and one draw needn't show every extreme that they name: legendre[m, l, t] is zero wherever l < m.
All inputs are finite; a program needn't handle non-finite values.
Results may differ from a plain program's by a relative error of at most 0.0068.
Values may be sent and summed in bfloat16 or wider, within the bound.
A program may use at most 64 MiB of HBM per device.

v0:
```python
import math

import jax
import jax.numpy as jnp
from jax import lax
from jax.sharding import Mesh
from jax.sharding import PartitionSpec as P

M = 384
LAT = ("lat_0", "lat_1", "lat_2")


def in_order(blocks, dim):
    shape = list(blocks.shape[1:])
    shape[dim] *= blocks.shape[0]
    return jnp.moveaxis(blocks, 0, dim).reshape(shape)


def from_everyone(x, axis):
    peers = lax.axis_size(axis)
    return lax.all_to_all(jnp.broadcast_to(x[None], (peers, *x.shape)), axis, 0, 0, tiled=True)


def collect(x, axis, dim):
    return in_order(from_everyone(x, axis), dim)


def in_blocks(x, dim, peers):
    before, after = (x.shape[:dim], x.shape[dim + 1 :])
    return jnp.moveaxis(x.reshape(*before, peers, -1, *after), dim, 0)


def turned_blocks(blocks, axes, turns):
    inside = blocks.shape[1:]
    whole = blocks.reshape(*(lax.axis_size(a) for a in axes), *inside)
    for k in turns:
        whole = lax.all_to_all(whole, axes[k], k, k, tiled=True)
    return whole.reshape(-1, *inside)


def exchange_by_chip(x, groups, turns, split_dim, concat_dim):
    peers = lax.axis_size(groups[0]) * lax.axis_size(groups[1])
    blocks = in_blocks(x, split_dim, peers)
    return in_order(turned_blocks(blocks, groups, turns), concat_dim)


def fourier_table(number, length):
    orders = jnp.arange(number, dtype=jnp.int32)
    points = jnp.arange(length, dtype=jnp.int32)
    phases = orders[:, None] * points[None, :] % length
    angles = phases.astype(jnp.float32) * (2.0 * math.pi / length)
    factor = 1.0 / math.sqrt(length)
    return jnp.stack([jnp.cos(angles) * factor, -jnp.sin(angles) * factor]).astype(jnp.bfloat16)


def body(grid_in, quad_weights, legendre, mixing):
    groups = grid_in.shape[0]
    rows_lat = grid_in.shape[1]
    length = grid_in.shape[2]
    fourier = fourier_table(M, length)
    spectra = jnp.einsum("ctn,rmn->mtrc", grid_in, fourier, preferred_element_type=jnp.float32)
    spectra = spectra * quad_weights[None, :, None, None]
    weighted = spectra.astype(jnp.bfloat16).reshape(M, rows_lat, 2 * groups)
    coeffs = jnp.einsum(
        "mlt,mtk->mlk",
        legendre,
        lax.all_to_all(weighted, LAT, split_axis=0, concat_axis=1, tiled=True),
        preferred_element_type=jnp.float32,
    ).astype(jnp.bfloat16)
    by_degree = lax.all_to_all(coeffs, LAT, split_axis=1, concat_axis=0, tiled=True)
    orders = by_degree.shape[0]
    degrees = by_degree.shape[1]
    weights_out = lax.all_to_all(mixing, "chan", split_axis=3, concat_axis=2, tiled=True)
    block_in = collect(by_degree, "chan", 2)
    shards = block_in.shape[2] // (2 * groups)
    halves = block_in.reshape(orders, degrees, shards, 2, groups)
    real_in = halves[:, :, :, 0, :].reshape(orders, degrees, shards * groups)
    imag_in = halves[:, :, :, 1, :].reshape(orders, degrees, shards * groups)
    real_weight = weights_out[0]
    imag_weight = weights_out[1]
    real_sum = jnp.einsum(
        "mlc,lcd->mld", real_in, real_weight, preferred_element_type=jnp.float32
    ) - jnp.einsum("mlc,lcd->mld", imag_in, imag_weight, preferred_element_type=jnp.float32)
    imag_sum = jnp.einsum(
        "mlc,lcd->mld", imag_in, real_weight, preferred_element_type=jnp.float32
    ) + jnp.einsum("mlc,lcd->mld", real_in, imag_weight, preferred_element_type=jnp.float32)
    mixed_coef = (
        jnp.stack([real_sum, imag_sum], axis=2)
        .reshape(orders, degrees, 2 * groups)
        .astype(jnp.bfloat16)
    )
    synthesis = jnp.einsum(
        "mlt,mlk->mtk",
        legendre,
        lax.all_to_all(mixed_coef, LAT, split_axis=0, concat_axis=1, tiled=True),
        preferred_element_type=jnp.float32,
    ).astype(jnp.bfloat16)
    gridded = exchange_by_chip(synthesis, (("lat_0", "lat_1"), "lat_2"), (1, 0), 1, 0)
    spread = gridded.reshape(M, rows_lat, 2, groups)
    restored = jnp.einsum("mtrc,rmn->ctn", spread, fourier, preferred_element_type=jnp.float32)
    return (restored + grid_in.astype(jnp.float32)).astype(jnp.bfloat16)


def solution(mesh):
    finer = Mesh(
        mesh.devices.reshape(8, 8, 2, mesh.shape["chan"]), ("lat_0", "lat_1", "lat_2", "chan")
    )
    placed = (P("chan", LAT, None), P(LAT), P(LAT, None, None), P(None, LAT, "chan", None))
    return jax.shard_map(
        body, mesh=finer, in_specs=placed, out_specs=P("chan", LAT, None), check_vma=False
    )
```

profile of v0, /device:TPU:1, one launch (start us, length us, event | category | flops | bytes accessed | tf_op | source)
XLA Modules:
  0.0 151.5 jit_solution(12542688453477254752)
XLA Ops:
  0.0 6.5 %multiply_convert_fusion = (bf16[1,384,1024]{2,1,0:T(8,128)(2,1)S(1)}, bf16[1,384,1024]{2,1,0:T(8,128)(2,1)S(1)}) fusion(), kind=kLoop, calls=%fused_computation.11 | loop fusion | flops 7471104 | bytes 1572864 | tf_op jit(solution)/shard_map/convert.7
  6.5 0.9 copy-done.1
  7.4 0.7 fusion.25
  8.1 0.2 copy.27
  8.4 36.1 %all_to_all.81 = bf16[384,3,128]{2,1,0:T(4,128)(2,1)S(1)} all-to-all(bf16[384,3,128]{2,1,0:T(4,128)(2,1)S(1)} %copy.27), channel_id=1, replica_groups=mesh['lat_0'=8,'lat_1'=8,'lat_2'=2,'chan'=4] {'lat_0','lat_1','lat_2'}, dimensions={0} | all-to-all | bytes 589824 | tf_op jit(solution)/shard_map/all_to_all | solution.py:67
  44.6 0.2 all_to_all.60
  44.8 0.5 fusion.28
  45.3 1.0 copy.31
  46.3 5.5 %all-to-all-start.1 = ((bf16[3,384,128]{2,0,1:T(4,128)(2,1)}), bf16[3,384,128]{2,0,1:T(4,128)(2,1)S(1)}, u32[]{:S(2)}, u32[]{:S(2)}) async-start(bf16[3,384,128]{2,0,1:T(4,128)(2,1)} %copy.31), calls=%async_computation.1 | async-start | bytes 786432 | tf_op jit(solution)/shard_map/all_to_all | solution.py:70
  51.8 0.3 copy.36
  52.1 1.0 reshape.101
  53.1 16.6 %all-to-all-done.1 = bf16[3,384,128]{2,0,1:T(4,128)(2,1)S(1)} async-done(((bf16[3,384,128]{2,0,1:T(4,128)(2,1)}), bf16[3,384,128]{2,0,1:T(4,128)(2,1)S(1)}, u32[]{:S(2)}, u32[]{:S(2)}) %all-to-all-start.1) | async-done | bytes 294944 | tf_op jit(solution)/shard_map/all_to_all | solution.py:70
  69.7 4.0 %all-to-all-start.3 = ((bf16[4,2,12288]{2,1,0:T(2,128)(2,1)}), bf16[4,2,12288]{2,1,0:T(2,128)(2,1)S(1)}, u32[]{:S(2)}, u32[]{:S(2)}) async-start(bf16[4,2,12288]{2,1,0:T(2,128)(2,1)} %reshape.101), calls=%async_computation.3 | async-start | bytes 393216 | tf_op jit(solution)/shard_map/all_to_all | solution.py:73
  73.9 0.2 broadcast_in_dim.4
  74.3 4.6 %all-to-all-done.3 = bf16[4,2,12288]{2,1,0:T(2,128)(2,1)S(1)} async-done(((bf16[4,2,12288]{2,1,0:T(2,128)(2,1)}), bf16[4,2,12288]{2,1,0:T(2,128)(2,1)S(1)}, u32[]{:S(2)}, u32[]{:S(2)}) %all-to-all-start.3) | async-done | bytes 196640 | tf_op jit(solution)/shard_map/all_to_all | solution.py:73
  78.9 1.2 broadcast_in_dim.5
  80.1 3.5 %all-to-all-start.2 = ((bf16[4,384,3,128]{1,3,2,0:T(8,128)(2,1)}), bf16[4,384,3,128]{1,3,2,0:T(8,128)(2,1)S(1)}, u32[]{:S(2)}, u32[]{:S(2)}) async-start(bf16[4,384,3,128]{1,3,2,0:T(8,128)(2,1)} %broadcast_in_dim.5), calls=%async_computation.2 | async-start | bytes 2359296 | tf_op jit(solution)/shard_map/all_to_all | solution.py:21
  83.6 1.3 reshape.102
  84.9 0.4 copy.69
  85.8 12.7 %all-to-all-done.2 = bf16[4,384,3,128]{1,3,2,0:T(8,128)(2,1)S(1)} async-done(((bf16[4,384,3,128]{1,3,2,0:T(8,128)(2,1)}), bf16[4,384,3,128]{1,3,2,0:T(8,128)(2,1)S(1)}, u32[]{:S(2)}, u32[]{:S(2)}) %all-to-all-start.2) | async-done | bytes 1179680 | tf_op jit(solution)/shard_map/all_to_all | solution.py:21
  99.0 0.2 fusion.41
  99.2 0.2 fusion.33
  99.5 0.2 fusion.32
  99.8 0.2 copy.43
  100.0 25.2 %all_to_all.82 = bf16[384,3,128]{2,1,0:T(4,128)(2,1)S(1)} all-to-all(bf16[384,3,128]{2,1,0:T(4,128)(2,1)S(1)} %copy.43), channel_id=1, replica_groups=mesh['lat_0'=8,'lat_1'=8,'lat_2'=2,'chan'=4] {'lat_0','lat_1','lat_2'}, dimensions={0} | all-to-all | bytes 589824 | tf_op jit(solution)/shard_map/all_to_all | solution.py:95
  125.4 0.2 all_to_all.71
  125.6 0.4 fusion.29
  126.5 3.9 %all_to_all.83 = bf16[64,2,3,3,128]{4,0,3,2,1:T(8,128)(2,1)S(1)} all-to-all(bf16[64,2,3,3,128]{4,0,3,2,1:T(8,128)(2,1)S(1)} %copy.48), channel_id=1, replica_groups=mesh['lat_0'=8,'lat_1'=8,'lat_2'=2,'chan'=4] {'lat_2'}, dimensions={1} | all-to-all | bytes 589824 | tf_op jit(solution)/shard_map/all_to_all | solution.py:37
  130.4 0.3 copy.49
  130.7 18.0 %all_to_all.84 = bf16[64,2,3,3,128]{4,1,3,2,0:T(2,128)(2,1)S(1)} all-to-all(bf16[64,2,3,3,128]{4,1,3,2,0:T(2,128)(2,1)S(1)} %copy.49), channel_id=1, replica_groups=mesh['lat_0'=8,'lat_1'=8,'lat_2'=2,'chan'=4] {'lat_0','lat_1'}, dimensions={0} | all-to-all | bytes 589824 | tf_op jit(solution)/shard_map/all_to_all | solution.py:37
  148.8 0.4 reshape_reshape_reshape.3
  149.2 2.3 %fusion.16 = bf16[64,3,1024]{2,0,1:T(8,128)(2,1)} fusion(bf16[1,384,1024]{2,1,0:T(8,128)(2,1)S(1)} %get-tuple-element.9, bf16[1,384,1024]{2,1,0:T(8,128)(2,1)S(1)} %copy-done.2, bf16[64,3,1024]{2,0,1:T(8,128)(2,1)} %param.4, bf16[384,3,2,64]{3,2,1,0:T(2,128)(2,1)S(1)} %reshape_reshape_reshape.3), kind=kOutput, calls=%fused_computation.18 | convolution fusion | flops 305725440 | bytes 2654208 | tf_op jit(solution)/shard_map/mtrc,rmn->ctn/dot_general | solution.py:100
  (30 shorter events, 2.3 us)
Async XLA Ops:
  0.0 44.8 %copy-start = (bf16[3,384,384]{2,1,0:T(8,128)(2,1)S(1)}, bf16[3,384,384]{2,1,0:T(8,128)(2,1)}, u32[]{:S(2)}) copy-start(bf16[3,384,384]{2,1,0:T(8,128)(2,1)} %param.6) | copy-start | bytes 2654212
  0.0 7.4 %copy-start.5 = (bf16[64,3,1024]{2,0,1:T(8,128)(2,1)S(1)}, bf16[64,3,1024]{2,0,1:T(8,128)(2,1)}, u32[]{:S(2)}) copy-start(bf16[64,3,1024]{2,0,1:T(8,128)(2,1)} %param.4) | copy-start | bytes 1179652
  0.0 7.4 %copy-start.6 = (f32[3]{0:T(128)S(1)}, f32[3]{0:T(128)}, u32[]{:S(2)}) copy-start(f32[3]{0:T(128)} %param.5) | copy-start | bytes 40
  6.5 0.9 copy-start.1
  44.8 6.9 %copy-start.4 = (bf16[2,3,64,256]{3,2,1,0:T(8,128)(2,1)S(1)}, bf16[2,3,64,256]{3,2,1,0:T(8,128)(2,1)}, u32[]{:S(2)}) copy-start(bf16[2,3,64,256]{3,2,1,0:T(8,128)(2,1)} %param.7) | copy-start | bytes 589828
  46.3 23.4 %all-to-all-start.1 = ((bf16[3,384,128]{2,0,1:T(4,128)(2,1)}), bf16[3,384,128]{2,0,1:T(4,128)(2,1)S(1)}, u32[]{:S(2)}, u32[]{:S(2)}) async-start(bf16[3,384,128]{2,0,1:T(4,128)(2,1)} %copy.31), calls=%async_computation.1 | async-start | bytes 786432 | tf_op jit(solution)/shard_map/all_to_all | solution.py:70
  69.7 9.2 %all-to-all-start.3 = ((bf16[4,2,12288]{2,1,0:T(2,128)(2,1)}), bf16[4,2,12288]{2,1,0:T(2,128)(2,1)S(1)}, u32[]{:S(2)}, u32[]{:S(2)}) async-start(bf16[4,2,12288]{2,1,0:T(2,128)(2,1)} %reshape.101), calls=%async_computation.3 | async-start | bytes 393216 | tf_op jit(solution)/shard_map/all_to_all | solution.py:73
  78.9 1.2 copy-start.3
  80.1 18.4 %all-to-all-start.2 = ((bf16[4,384,3,128]{1,3,2,0:T(8,128)(2,1)}), bf16[4,384,3,128]{1,3,2,0:T(8,128)(2,1)S(1)}, u32[]{:S(2)}, u32[]{:S(2)}) async-start(bf16[4,384,3,128]{1,3,2,0:T(8,128)(2,1)} %broadcast_in_dim.5), calls=%async_computation.2 | async-start | bytes 2359296 | tf_op jit(solution)/shard_map/all_to_all | solution.py:21
  130.7 18.5 %copy-start.2 = (bf16[1,384,1024]{2,1,0:T(8,128)(2,1)S(1)}, bf16[1,384,1024]{2,1,0:T(8,128)(2,1)}, u32[]{:S(2)}) copy-start(bf16[1,384,1024]{2,1,0:T(8,128)(2,1)} %copy-done.1) | copy-start | bytes 2359300
where the time goes:
time: 153 us; the launch traced here: 151 us
  blocking collectives  83.2 us (54%)
  waiting for transfers between devices  33.9 us (22%)
  starting transfers between devices  13 us (8%)
  local copies, waits for them, and re-layouts  9.87 us (6%)
  other arithmetic  6.49 us (4%)
  matrix products  4.73 us (3%)
    all_to_all x1, blocking collectives, body(): lax.all_to_all(weighted, LAT, split_axis=0, concat_axis=1, tiled=True)  36.1 us
    all_to_all x1, blocking collectives, body(): lax.all_to_all(mixed_coef, LAT, split_axis=0, concat_axis=1, tiled=True)  25.2 us
    all_to_all x2, blocking collectives, turned_blocks(): whole = lax.all_to_all(whole, axes[k], k, k, tiled=True)  21.9 us
    all_to_all x1, waiting for transfers between devices, body(): lax.all_to_all(coeffs, LAT, split_axis=1, concat_axis=0, tiled=True)  16.6 us
    all_to_all x1, waiting for transfers between devices, from_everyone(): lax.all_to_all(jnp.broadcast_to(x[None], (peers, *x.shape)), axis, 0, 0,...  12.7 us
    another operation x1, other arithmetic  6.45 us
    all_to_all x1, starting transfers between devices, body(): lax.all_to_all(coeffs, LAT, split_axis=1, concat_axis=0, tiled=True)  5.47 us
    all_to_all x1, waiting for transfers between devices, body(): lax.all_to_all(mixing, 'chan', split_axis=3, concat_axis=2, tiled=True)  4.62 us
  transfers between devices with their start and end apart: 3, of which 3 were waited for; matrix products, arithmetic and copies ran while one was open for 3% of the time, Pallas kernels for 0%

commit v1 on v0

v1 whole, which is shorter than its diff:
```python
import functools

import jax
import jax.numpy as jnp
import numpy as np
from jax import lax
from jax.experimental import pallas as pl
from jax.experimental.pallas import tpu as pltpu
from jax.sharding import PartitionSpec as P

MESH = pl.DeviceIdType.MESH
BF = jnp.bfloat16
F32 = jnp.float32


def fourier_rows(peers, length):
    slot = np.arange(2 * peers)
    near, far = 3 * (slot // 2) + slot % 2, 3 * (slot // 2) + 2
    points = np.arange(length)
    factor = np.float32(1.0 / np.sqrt(length))
    parts = []
    for orders in (near, far):
        phases = (orders[:, None] * points[None, :]) % length
        angles = phases.astype(np.float32) * np.float32(2.0 * np.pi / length)
        parts += [np.cos(angles) * factor, -np.sin(angles) * factor]
    return np.concatenate(parts).astype(BF)


def nt(a, b):
    return lax.dot_general(a, b, (((1,), (1,)), ((), ())), preferred_element_type=F32)


def nn(a, b):
    return jnp.dot(a, b, preferred_element_type=F32)


def kernel(
    peers, chans, grid_z, grid_y,
    x_hbm, quad, leg_hbm, mix_hbm, tab_hbm, out_hbm,
    x, leg, tab, picks, tables, turned, weights, mixer,
    send_a, got_a, send_b, got_b, send_c, got_c, send_d, got_d,
    spread_rows, total, result,
    load_sem, snd, rcv, w_snd, w_rcv,
):
    me, chan = lax.axis_index("lat"), lax.axis_index("chan")
    rows = 2 * peers
    width = x.shape[1]
    near, far = slice(0, 3), slice(3, 5)
    group = peers // chans
    pair_of = lambda p: pl.ds(2 * p, 2)
    stacked = lambda ref, part: ref[part].reshape(-1, 128)

    loads = [
        pltpu.make_async_copy(x_hbm, x, load_sem.at[0]),
        pltpu.make_async_copy(tab_hbm, tab, load_sem.at[1]),
        pltpu.make_async_copy(leg_hbm, leg, load_sem.at[2]),
        pltpu.make_async_copy(mix_hbm, weights.at[chan], load_sem.at[3]),
    ]
    for load in loads:
        load.start()

    core, y, z = lax.rem(me, 2), lax.rem(lax.div(me, 2), grid_y), lax.div(me, 2 * grid_y)

    def far_first(k, n):
        return lax.rem(n // 2 + (1 - 2 * lax.rem(k, 2)) * lax.div(k + 1, 2), n)

    def peer_of(k):
        pz = lax.rem(z + far_first(lax.div(k, 2 * grid_y), grid_z), grid_z)
        py = lax.rem(y + far_first(lax.rem(lax.div(k, 2), grid_y), grid_y), grid_y)
        return (pz * grid_y + py) * 2 + lax.rem(core + 1 + lax.rem(k, 2), 2)

    barrier = pltpu.get_barrier_semaphore()

    @pl.loop(0, peers - 1)
    def _(k):
        pl.semaphore_signal(barrier, inc=1, device_id=(peer_of(k), chan), device_id_type=MESH)

    for d in range(1, chans):
        pl.semaphore_signal(barrier, inc=1, device_id=(me, lax.rem(chan + d, chans)), device_id_type=MESH)

    slot = lax.broadcasted_iota(jnp.int32, (rows, 3 * peers), 0)
    column = lax.broadcasted_iota(jnp.int32, (rows, 3 * peers), 1)
    base = 3 * (slot >> 1)
    odd = (slot & 1) == 1
    one = lambda mask: jnp.where(mask, 1.0, 0.0).astype(BF)
    for u in range(3):
        hit = column == base + u
        picks[0, u * rows : (u + 1) * rows] = one(hit & jnp.logical_not(odd))
        picks[1, u * rows : (u + 1) * rows] = one(hit & odd)
    picks[2, 0:rows] = one(column == base + (slot & 1))
    picks[2, rows : 2 * rows] = one((column == base + 2) & jnp.logical_not(odd))

    loads[0].wait()
    loads[1].wait()
    points = x[...].reshape(3 * width, x.shape[2])
    odd_row = (lax.broadcasted_iota(jnp.int32, (rows, 128), 0) & 1) == 1

    def waves(part):
        real = nt(tab[2 * part * rows : (2 * part + 1) * rows], points)
        imag = nt(tab[(2 * part + 1) * rows : (2 * part + 2) * rows], points)
        return [
            jnp.concatenate(
                [real[:, u * width : (u + 1) * width], imag[:, u * width : (u + 1) * width]], axis=1
            )
            * quad[u]
            for u in range(3)
        ]

    for u, value in enumerate(waves(0)):
        send_a[u] = value.astype(BF)
    first, second, third = waves(1)
    send_a[3] = jnp.where(odd_row, second, first).astype(BF)
    send_a[4] = jnp.where(odd_row, 0.0, third).astype(BF)

    loads[3].wait()
    pl.semaphore_wait(barrier, peers - 1 + chans - 1)

    def send_lat(src, dst, which):
        for g, part in enumerate((near, far)):
            sem = 2 * which + g

            @pl.loop(0, peers - 1)
            def _(k):
                p = peer_of(k)
                pltpu.make_async_remote_copy(
                    src_ref=src.at[part, pair_of(p)], dst_ref=dst.at[part, pair_of(me)],
                    send_sem=snd.at[sem], recv_sem=rcv.at[sem],
                    device_id=(p, chan), device_id_type=MESH,
                ).start()

            pltpu.make_async_copy(src.at[part, pair_of(me)], dst.at[part, pair_of(me)], rcv.at[sem]).start()
            yield

    def forward(src_ref, dst_ref, sem, target_lat, target_chan):
        here = jnp.logical_and(target_lat == me, target_chan == chan)

        @pl.when(here)
        def _():
            pltpu.make_async_copy(src_ref, dst_ref, rcv.at[sem]).start()

        @pl.when(jnp.logical_not(here))
        def _():
            pltpu.make_async_remote_copy(
                src_ref=src_ref, dst_ref=dst_ref, send_sem=snd.at[sem], recv_sem=rcv.at[sem],
                device_id=(target_lat, target_chan), device_id_type=MESH,
            ).start()

    def arrived(dst, which, g):
        part = (near, far)[g]
        pltpu.make_async_copy(dst.at[part], dst.at[part], rcv.at[2 * which + g]).wait()

    for _ in send_lat(send_a, got_a, 0):
        pass
    for d in range(1, chans):
        pltpu.make_async_remote_copy(
            src_ref=weights.at[chan], dst_ref=weights.at[chan],
            send_sem=w_snd.at[d - 1], recv_sem=w_rcv.at[d - 1],
            device_id=(me, lax.rem(chan + d, chans)), device_id_type=MESH,
        ).start()

    loads[2].wait()
    for u in range(3):
        at = slice(u * rows, (u + 1) * rows)
        value = 0.0
        for h in range(2):
            picked = nn(picks[h, at], leg[h]).astype(BF)
            value = value + nt(picked, picks[h])
        tables[0, at] = value.astype(BF)
    for q in range(2):
        at = slice(q * rows, (q + 1) * rows)
        picked = nn(picks[2, at], leg[2]).astype(BF)
        tables[1, at, 0 : 2 * rows] = nt(picked, picks[2, 0 : 2 * rows]).astype(BF)

    def send_degrees(g):
        part = (near, far)[g]
        own = lax.div(me, chans)

        @pl.loop(0, peers)
        def _(k):
            p = peer_of(k)
            forward(send_b.at[part, pair_of(p)], got_b.at[part, chan, pair_of(own)], 2 + g, p, lax.rem(me + p, chans))

    arrived(got_a, 0, 0)
    send_b[near] = nn(tables[0], stacked(got_a, near)).astype(BF).reshape(3, rows, 128)
    send_degrees(0)
    arrived(got_a, 0, 1)
    few = slice(0, 2 * rows)
    send_b[far] = nn(tables[1, few, few], stacked(got_a, far)).astype(BF).reshape(2, rows, 128)
    send_degrees(1)

    for u in range(3):
        at = slice(u * rows, (u + 1) * rows)
        value = 0.0
        for h in range(2):
            picked = nt(picks[h, at], leg[h]).astype(BF)
            value = value + nt(picked, picks[h])
        turned[0, at] = value.astype(BF)
    for q in range(2):
        at = slice(q * rows, (q + 1) * rows)
        picked = nt(picks[2, at], leg[2]).astype(BF)
        turned[1, at, 0 : 2 * rows] = nt(picked, picks[2, 0 : 2 * rows]).astype(BF)

    for d in range(1, chans):
        source = lax.rem(chan + chans - d, chans)
        pltpu.make_async_copy(weights.at[source], weights.at[source], w_rcv.at[d - 1]).wait()
    for degree in range(3):
        for c in range(chans):
            real, imag = weights[c, 0, degree], weights[c, 1, degree]
            upper, lower = [], []
            for d in range(chans):
                cut = slice(d * width, (d + 1) * width)
                upper += [real[:, cut], imag[:, cut]]
                lower += [-imag[:, cut], real[:, cut]]
            top = c * 2 * width
            mixer[degree, top : top + width] = jnp.concatenate(upper, axis=1)
            mixer[degree, top + width : top + 2 * width] = jnp.concatenate(lower, axis=1)

    some = 2 * group

    def values_of(q):
        return jnp.concatenate([got_b[q, c] for c in range(chans)], axis=1)

    def put_mixed(q, value):
        for d in range(chans):
            send_c[q, d] = value[:, d * 128 : (d + 1) * 128].astype(BF)

    def send_orders(g):
        part = (near, far)[g]
        shift = lax.rem(chan + peers - lax.rem(me, chans), chans)
        own = lax.div(me, chans)

        @pl.loop(0, peers)
        def _(k):
            d = lax.rem(chan + 2 + lax.rem(k, chans), chans)
            turn = lax.rem(own + group // 2 + lax.div(k, chans), group)
            forward(send_c.at[part, d, pair_of(turn)], got_c.at[part, pair_of(me)], 4 + g, turn * chans + shift, d)

    arrived(got_b, 1, 0)
    for u in range(3):
        put_mixed(u, nn(values_of(u), mixer[u]))
    send_orders(0)
    arrived(got_b, 1, 1)
    both = values_of(3)
    odd_some = (lax.broadcasted_iota(jnp.int32, (some, chans * 128), 0) & 1) == 1
    put_mixed(3, jnp.where(odd_some, nn(both, mixer[1]), nn(both, mixer[0])))
    put_mixed(4, nn(values_of(4), mixer[2]))
    send_orders(1)

    back = send_lat(send_d, got_d, 3)
    arrived(got_c, 2, 0)
    send_d[near] = nn(turned[0], stacked(got_c, near)).astype(BF).reshape(3, rows, 128)
    next(back)
    arrived(got_c, 2, 1)
    send_d[far] = nn(turned[1, few, few], stacked(got_c, far)).astype(BF).reshape(2, rows, 128)
    next(back)

    odd_lane = (lax.broadcasted_iota(jnp.int32, (128, rows), 1) & 1) == 1
    arrived(got_d, 3, 0)
    for u in range(3):
        at = slice(u * width, (u + 1) * width)
        flipped = got_d[u].T
        spread_rows[at, 0:rows] = flipped[0:width]
        spread_rows[at, rows : 2 * rows] = flipped[width : 2 * width]
    total[...] = points.astype(F32) + nn(spread_rows[:, 0 : 2 * rows], tab[0 : 2 * rows])
    arrived(got_d, 3, 1)
    pair = got_d[3].T
    zero = jnp.zeros_like(pair)
    last = got_d[4].T
    for u, value in enumerate((jnp.where(odd_lane, zero, pair), jnp.where(odd_lane, pair, zero), jnp.where(odd_lane, zero, last))):
        at = slice(u * width, (u + 1) * width)
        spread_rows[at, 2 * rows : 3 * rows] = value[0:width]
        spread_rows[at, 3 * rows : 4 * rows] = value[width : 2 * width]
    done = total[...] + nn(spread_rows[:, 2 * rows : 4 * rows], tab[2 * rows : 4 * rows])
    result[...] = done.astype(BF).reshape(result.shape)
    store = pltpu.make_async_copy(result, out_hbm, load_sem.at[4])
    store.start()

    own_target = lax.rem(2 * me, chans) == chan
    for which, buffer in ((0, send_a), (1, send_a), (2, send_a), (3, send_a)):
        for g, part in enumerate((near, far)):
            sem = snd.at[2 * which + g]
            sent = buffer.at[part, pl.ds(0, rows - 2)]
            pltpu.make_async_copy(sent, sent, sem).wait()
            if which in (1, 2):
                extra = buffer.at[part, pl.ds(0, 2)]

                @pl.when(jnp.logical_not(own_target))
                def _():
                    pltpu.make_async_copy(extra, extra, sem).wait()

    for d in range(1, chans):
        pltpu.make_async_copy(weights.at[chan], weights.at[chan], w_snd.at[d - 1]).wait()
    store.wait()


def body(peers, chans, grid_z, grid_y, grid_in, quad_weights, legendre, mixing):
    width, _, length = grid_in.shape
    rows = 2 * peers
    table = jnp.asarray(fourier_rows(peers, length))
    plain = pltpu.VMEM((5, rows, 128), BF)
    split = pltpu.VMEM((5, chans, rows // chans, 128), BF)
    anywhere = pl.BlockSpec(memory_space=pl.ANY)
    dma = pltpu.SemaphoreType.DMA
    out = pl.pallas_call(
        functools.partial(kernel, peers, chans, grid_z, grid_y),
        out_shape=jax.ShapeDtypeStruct((3, width, length), BF),
        in_specs=[anywhere, pl.BlockSpec(memory_space=pltpu.SMEM), anywhere, anywhere, anywhere],
        out_specs=anywhere,
        scratch_shapes=[
            pltpu.VMEM((3, width, length), BF),
            pltpu.VMEM(legendre.shape, BF),
            pltpu.VMEM((4 * rows, length), BF),
            pltpu.VMEM((3, 3 * rows, 3 * peers), BF),
            pltpu.VMEM((2, 3 * rows, 3 * rows), BF),
            pltpu.VMEM((2, 3 * rows, 3 * rows), BF),
            pltpu.VMEM((chans, *mixing.shape), BF),
            pltpu.VMEM((3, chans * 2 * width, chans * 2 * width), BF),
            plain, plain, plain, split, split, plain, plain, plain,
            pltpu.VMEM((3 * width, 4 * rows), BF),
            pltpu.VMEM((3 * width, length), F32),
            pltpu.VMEM((3, width, length), BF),
            dma((5,)), dma((8,)), dma((8,)), dma((chans - 1,)), dma((chans - 1,)),
        ],
        compiler_params=pltpu.CompilerParams(
            collective_id=0, has_side_effects=True, vmem_limit_bytes=48 * 1024 * 1024
        ),
    )(grid_in.transpose(1, 0, 2), quad_weights, legendre, mixing, table)
    return out.transpose(1, 0, 2)


def solution(mesh):
    peers, chans = mesh.shape["lat"], mesh.shape["chan"]
    grid_y = grid_z = int(round((peers // 2) ** 0.5))
    return jax.shard_map(
        functools.partial(body, peers, chans, grid_z, grid_y),
        mesh=mesh,
        in_specs=(P("chan", "lat", None), P("lat"), P("lat", None, None), P(None, "lat", "chan", None)),
        out_specs=P("chan", "lat", None),
        check_vma=False,
    )
```

time: 153 us -> 84.9 us (0.55)
  blocking collectives: 83.2 us -> 0 us
  Pallas kernels: 0 us -> 78.5 us
  waiting for transfers between devices: 33.9 us -> 0 us
  starting transfers between devices: 13 us -> 0 us
  other arithmetic: 6.49 us -> 0 us
  matrix products: 4.73 us -> 0 us
  local copies, waits for them, and re-layouts: 9.87 us -> 6.08 us
    all_to_all x4 -> x0, blocking collectives: 83.2 us -> none  [the longest x1 36.1 us: body(): lax.all_to_all(weighted, LAT, split_axis=0, concat_axis=1, tiled=True)]
    pallas_call x0 -> x1, Pallas kernels: none -> 78.5 us  [body(): pl.pallas_call(functools.partial(kernel, peers, chans, grid_z, grid_y), o...]
    all_to_all x3 -> x0, waiting for transfers between devices: 33.9 us -> none  [the longest x1 16.6 us: body(): lax.all_to_all(coeffs, LAT, split_axis=1, concat_axis=0, tiled=True)]
    all_to_all x3 -> x0, starting transfers between devices: 13 us -> none  [the longest x1 5.47 us: body(): lax.all_to_all(coeffs, LAT, split_axis=1, concat_axis=0, tiled=True)]
    another operation x2 -> x0, other arithmetic: 6.49 us -> none
    dot_general x8 -> x0, matrix products: 4.73 us -> none  [the longest x1 2.27 us: body(): jnp.einsum('mtrc,rmn->ctn', spread, fourier, preferred_element_type=jnp.f...]
    unnamed x17 -> x11, local copies, waits for them, and re-layouts: 3.54 us -> 6.08 us
    all_to_all x9 -> x0, local copies, waits for them, and re-layouts: 1.8 us -> none  [the longest x2 0.42 us: turned_blocks(): whole = lax.all_to_all(whole, axes[k], k, k, tiled=True)]
  transfers between devices with their start and end apart: 3 -> 0, of which waited for: 3 -> 0; matrix products, arithmetic and copies ran while one was open for 3% -> 0% of each run, Pallas kernels for 0% -> 0%
where the time goes in v1:
time: 84.9 us; the launch traced here: 84.6 us
  Pallas kernels  78.5 us (92%)
  local copies, waits for them, and re-layouts  6.08 us (7%)
    pallas_call x1, Pallas kernels, body(): pl.pallas_call(functools.partial(kernel, peers, chans, grid_z, grid_y), o...  78.5 us
    unnamed x11, local copies, waits for them, and re-layouts  6.08 us

profile of v1, /device:TPU:1, one launch (start us, length us, event | category | flops | bytes accessed | tf_op | source)
XLA Modules:
  0.0 84.6 jit_solution(16522864193829042346)
XLA Ops:
  0.0 0.0 copy-start
  0.0 1.6 %copy-done = bf16[1024,1024]{1,0:T(8,128)(2,1)S(1)} copy-done((bf16[1024,1024]{1,0:T(8,128)(2,1)S(1)}, bf16[1024,1024]{1,0:T(8,128)(2,1)}, u32[]{:S(2)}) %copy-start) | copy-done | bytes 2097176
  1.6 0.0 copy-start.1
  1.6 1.2 %copy-done.1 = bf16[3,384,384]{2,1,0:T(8,128)(2,1)S(1)} copy-done((bf16[3,384,384]{2,1,0:T(8,128)(2,1)S(1)}, bf16[3,384,384]{2,1,0:T(8,128)(2,1)}, u32[]{:S(2)}) %copy-start.1) | copy-done | bytes 884760
  2.8 0.0 copy-start.2
  2.8 1.0 %copy-done.2 = bf16[64,3,1024]{2,0,1:T(8,128)(2,1)S(1)} copy-done((bf16[64,3,1024]{2,0,1:T(8,128)(2,1)S(1)}, bf16[64,3,1024]{2,0,1:T(8,128)(2,1)}, u32[]{:S(2)}) %copy-start.2) | copy-done | bytes 393240
  3.8 0.0 copy-start.3
  3.8 0.9 %copy-done.3 = bf16[2,3,64,256]{3,2,1,0:T(8,128)(2,1)S(1)} copy-done((bf16[2,3,64,256]{3,2,1,0:T(8,128)(2,1)S(1)}, bf16[2,3,64,256]{3,2,1,0:T(8,128)(2,1)}, u32[]{:S(2)}) %copy-start.3) | copy-done | bytes 196632
  4.7 0.0 copy-start.4
  4.7 0.7 copy-done.4
  5.3 78.5 %shard_map.55 = bf16[3,64,1024]{2,1,0:T(8,128)(2,1)S(1)} custom-call(bf16[3,64,1024]{2,1,0:T(8,128)(2,1)S(1)} %bitcast.3, f32[3]{0:T(128)S(1)} %copy-done.4, bf16[3,384,384]{2,1,0:T(8,128)(2,1)S(1)} %copy-done.1, bf16[2,3,64,256]{3,2,1,0:T(8,128)(2,1)S(1)} %copy-done.3, bf16[1024,1024]{1,0:T(8,128)(2,1)S(1)} %copy-done), custom_call_target="tpu_custom_call" | custom-call | tf_op jit(solution)/shard_map/pallas_call | solution.py:304
  83.8 0.7 copy.7
Async XLA Ops:
  0.0 1.6 %copy-start = (bf16[1024,1024]{1,0:T(8,128)(2,1)S(1)}, bf16[1024,1024]{1,0:T(8,128)(2,1)}, u32[]{:S(2)}) copy-start(bf16[1024,1024]{1,0:T(8,128)(2,1)} %constant.2.clone.tab_hbm) | copy-start | bytes 6291460
  1.6 1.2 %copy-start.1 = (bf16[3,384,384]{2,1,0:T(8,128)(2,1)S(1)}, bf16[3,384,384]{2,1,0:T(8,128)(2,1)}, u32[]{:S(2)}) copy-start(bf16[3,384,384]{2,1,0:T(8,128)(2,1)} %leg_hbm.1) | copy-start | bytes 2654212
  2.8 1.0 %copy-start.2 = (bf16[64,3,1024]{2,0,1:T(8,128)(2,1)S(1)}, bf16[64,3,1024]{2,0,1:T(8,128)(2,1)}, u32[]{:S(2)}) copy-start(bf16[64,3,1024]{2,0,1:T(8,128)(2,1)} %param.5) | copy-start | bytes 1179652
  3.8 0.9 %copy-start.3 = (bf16[2,3,64,256]{3,2,1,0:T(8,128)(2,1)S(1)}, bf16[2,3,64,256]{3,2,1,0:T(8,128)(2,1)}, u32[]{:S(2)}) copy-start(bf16[2,3,64,256]{3,2,1,0:T(8,128)(2,1)} %mix_hbm.1) | copy-start | bytes 589828
  4.7 0.7 copy-start.4

commit v2 on v1

--- a/solution.py
+++ b/solution.py
@@ -35,11 +35,11 @@
 
 
 def kernel(
-    peers, chans, grid_z, grid_y,
-    x_hbm, quad, leg_hbm, mix_hbm, tab_hbm, out_hbm,
+    peers, chans,
+    x_hbm, quad, leg_hbm, mix_hbm, tab_hbm, result,
     x, leg, tab, picks, tables, turned, weights, mixer,
     send_a, got_a, send_b, got_b, send_c, got_c, send_d, got_d,
-    spread_rows, total, result,
+    spread_rows, total,
     load_sem, snd, rcv, w_snd, w_rcv,
 ):
     me, chan = lax.axis_index("lat"), lax.axis_index("chan")
@@ -59,21 +59,14 @@
     for load in loads:
         load.start()
 
-    core, y, z = lax.rem(me, 2), lax.rem(lax.div(me, 2), grid_y), lax.div(me, 2 * grid_y)
-
-    def far_first(k, n):
-        return lax.rem(n // 2 + (1 - 2 * lax.rem(k, 2)) * lax.div(k + 1, 2), n)
-
-    def peer_of(k):
-        pz = lax.rem(z + far_first(lax.div(k, 2 * grid_y), grid_z), grid_z)
-        py = lax.rem(y + far_first(lax.rem(lax.div(k, 2), grid_y), grid_y), grid_y)
-        return (pz * grid_y + py) * 2 + lax.rem(core + 1 + lax.rem(k, 2), 2)
+    def wrap(value, n):
+        return jnp.where(value >= n, value - n, value)
 
     barrier = pltpu.get_barrier_semaphore()
 
-    @pl.loop(0, peers - 1)
+    @pl.loop(1, peers, unroll=4)
     def _(k):
-        pl.semaphore_signal(barrier, inc=1, device_id=(peer_of(k), chan), device_id_type=MESH)
+        pl.semaphore_signal(barrier, inc=1, device_id=(wrap(me + k, peers), chan), device_id_type=MESH)
 
     for d in range(1, chans):
         pl.semaphore_signal(barrier, inc=1, device_id=(me, lax.rem(chan + d, chans)), device_id_type=MESH)
@@ -119,9 +112,9 @@
         for g, part in enumerate((near, far)):
             sem = 2 * which + g
 
-            @pl.loop(0, peers - 1)
+            @pl.loop(1, peers, unroll=4)
             def _(k):
-                p = peer_of(k)
+                p = wrap(me + k, peers)
                 pltpu.make_async_remote_copy(
                     src_ref=src.at[part, pair_of(p)], dst_ref=dst.at[part, pair_of(me)],
                     send_sem=snd.at[sem], recv_sem=rcv.at[sem],
@@ -132,6 +125,12 @@
             yield
 
     def forward(src_ref, dst_ref, sem, target_lat, target_chan):
+        pltpu.make_async_remote_copy(
+            src_ref=src_ref, dst_ref=dst_ref, send_sem=snd.at[sem], recv_sem=rcv.at[sem],
+            device_id=(target_lat, target_chan), device_id_type=MESH,
+        ).start()
+
+    def forward_near(src_ref, dst_ref, sem, target_lat, target_chan):
         here = jnp.logical_and(target_lat == me, target_chan == chan)
 
         @pl.when(here)
@@ -140,10 +139,7 @@
 
         @pl.when(jnp.logical_not(here))
         def _():
-            pltpu.make_async_remote_copy(
-                src_ref=src_ref, dst_ref=dst_ref, send_sem=snd.at[sem], recv_sem=rcv.at[sem],
-                device_id=(target_lat, target_chan), device_id_type=MESH,
-            ).start()
+            forward(src_ref, dst_ref, sem, target_lat, target_chan)
 
     def arrived(dst, which, g):
         part = (near, far)[g]
@@ -173,12 +169,20 @@
 
     def send_degrees(g):
         part = (near, far)[g]
-        own = lax.div(me, chans)
-
-        @pl.loop(0, peers)
+        landing = got_b.at[part, chan, pair_of(lax.div(me, chans))]
+        meets = [lax.rem(2 * me + r, chans) for r in range(chans)]
+
+        def one(how, k, r):
+            p = wrap(me + k, peers)
+            how(send_b.at[part, pair_of(p)], landing, 2 + g, p, meets[r])
+
+        @pl.loop(1, peers // chans)
         def _(k):
-            p = peer_of(k)
-            forward(send_b.at[part, pair_of(p)], got_b.at[part, chan, pair_of(own)], 2 + g, p, lax.rem(me + p, chans))
+            for r in range(chans):
+                one(forward, k * chans + r, r)
+
+        for r in range(chans):
+            one(forward if r else forward_near, r, r)
 
     arrived(got_a, 0, 0)
     send_b[near] = nn(tables[0], stacked(got_a, near)).astype(BF).reshape(3, rows, 128)
@@ -229,11 +233,18 @@
         shift = lax.rem(chan + peers - lax.rem(me, chans), chans)
         own = lax.div(me, chans)
 
-        @pl.loop(0, peers)
+        landing = got_c.at[part, pair_of(me)]
+
+        def one(how, k):
+            turn = wrap(own + k, group)
+            for d in range(chans):
+                how(send_c.at[part, d, pair_of(turn)], landing, 4 + g, turn * chans + shift, d)
+
+        @pl.loop(1, group)
         def _(k):
-            d = lax.rem(chan + 2 + lax.rem(k, chans), chans)
-            turn = lax.rem(own + group // 2 + lax.div(k, chans), group)
-            forward(send_c.at[part, d, pair_of(turn)], got_c.at[part, pair_of(me)], 4 + g, turn * chans + shift, d)
+            one(forward, k)
+
+        one(forward_near, 0)
 
     arrived(got_b, 1, 0)
     for u in range(3):
@@ -272,8 +283,6 @@
         spread_rows[at, 3 * rows : 4 * rows] = value[width : 2 * width]
     done = total[...] + nn(spread_rows[:, 2 * rows : 4 * rows], tab[2 * rows : 4 * rows])
     result[...] = done.astype(BF).reshape(result.shape)
-    store = pltpu.make_async_copy(result, out_hbm, load_sem.at[4])
-    store.start()
 
     own_target = lax.rem(2 * me, chans) == chan
     for which, buffer in ((0, send_a), (1, send_a), (2, send_a), (3, send_a)):
@@ -290,22 +299,21 @@
 
     for d in range(1, chans):
         pltpu.make_async_copy(weights.at[chan], weights.at[chan], w_snd.at[d - 1]).wait()
-    store.wait()
-
-
-def body(peers, chans, grid_z, grid_y, grid_in, quad_weights, legendre, mixing):
+
+
+def body(peers, chans, grid_in, quad_weights, legendre, mixing):
     width, _, length = grid_in.shape
     rows = 2 * peers
     table = jnp.asarray(fourier_rows(peers, length))
     plain = pltpu.VMEM((5, rows, 128), BF)
     split = pltpu.VMEM((5, chans, rows // chans, 128), BF)
-    anywhere = pl.BlockSpec(memory_space=pl.ANY)
+    stay = pl.BlockSpec(memory_space=pltpu.HBM)
     dma = pltpu.SemaphoreType.DMA
     out = pl.pallas_call(
-        functools.partial(kernel, peers, chans, grid_z, grid_y),
+        functools.partial(kernel, peers, chans),
         out_shape=jax.ShapeDtypeStruct((3, width, length), BF),
-        in_specs=[anywhere, pl.BlockSpec(memory_space=pltpu.SMEM), anywhere, anywhere, anywhere],
-        out_specs=anywhere,
+        in_specs=[stay, pl.BlockSpec(memory_space=pltpu.SMEM), stay, stay, stay],
+        out_specs=pl.BlockSpec(memory_space=pltpu.VMEM),
         scratch_shapes=[
             pltpu.VMEM((3, width, length), BF),
             pltpu.VMEM(legendre.shape, BF),
@@ -318,11 +326,10 @@
             plain, plain, plain, split, split, plain, plain, plain,
             pltpu.VMEM((3 * width, 4 * rows), BF),
             pltpu.VMEM((3 * width, length), F32),
-            pltpu.VMEM((3, width, length), BF),
-            dma((5,)), dma((8,)), dma((8,)), dma((chans - 1,)), dma((chans - 1,)),
+            dma((4,)), dma((8,)), dma((8,)), dma((chans - 1,)), dma((chans - 1,)),
         ],
         compiler_params=pltpu.CompilerParams(
-            collective_id=0, has_side_effects=True, vmem_limit_bytes=48 * 1024 * 1024
+            collective_id=0, has_side_effects=True, vmem_limit_bytes=67043328
         ),
     )(grid_in.transpose(1, 0, 2), quad_weights, legendre, mixing, table)
     return out.transpose(1, 0, 2)
@@ -330,9 +337,8 @@
 
 def solution(mesh):
     peers, chans = mesh.shape["lat"], mesh.shape["chan"]
-    grid_y = grid_z = int(round((peers // 2) ** 0.5))
     return jax.shard_map(
-        functools.partial(body, peers, chans, grid_z, grid_y),
+        functools.partial(body, peers, chans),
         mesh=mesh,
         in_specs=(P("chan", "lat", None), P("lat"), P("lat", None, None), P(None, "lat", "chan", None)),
         out_specs=P("chan", "lat", None),

time: 84.9 us -> 67.3 us (0.79)
  Pallas kernels: 78.5 us -> 65.4 us
  local copies, waits for them, and re-layouts: 6.08 us -> 1.77 us
    pallas_call x1, Pallas kernels: 78.5 us -> 65.4 us  [body(): pl.pallas_call(functools.partial(kernel, peers, chans), out_shape=jax.Sha...]
    unnamed x11 -> x1, local copies, waits for them, and re-layouts: 6.08 us -> 1.77 us
where the time goes in v2:
time: 67.3 us; the launch traced here: 67.1 us
  Pallas kernels  65.4 us (97%)
  local copies, waits for them, and re-layouts  1.77 us (3%)
    pallas_call x1, Pallas kernels, body(): pl.pallas_call(functools.partial(kernel, peers, chans), out_shape=jax.Sha...  65.4 us
    unnamed x1, local copies, waits for them, and re-layouts  1.77 us

profile of v2, /device:TPU:1, one launch (start us, length us, event | category | flops | bytes accessed | tf_op | source)
XLA Modules:
  0.0 67.1 jit_solution(7665758343735291294)
XLA Ops:
  0.0 65.4 %shard_map.55 = bf16[3,64,1024]{2,1,0:T(8,128)(2,1)} custom-call(bf16[3,64,1024]{2,1,0:T(8,128)(2,1)} %bitcast.3, f32[3]{0:T(128)} %quad.1, bf16[3,384,384]{2,1,0:T(8,128)(2,1)} %leg_hbm.1, bf16[2,3,64,256]{3,2,1,0:T(8,128)(2,1)} %mix_hbm.1, bf16[1024,1024]{1,0:T(8,128)(2,1)} %constant.2.clone.tab_hbm), custom_call_target="tpu_custom_call" | custom-call | tf_op jit(solution)/shard_map/pallas_call | solution.py:312
  65.4 1.8 %copy.7 = bf16[64,3,1024]{2,0,1:T(8,128)(2,1)} copy(bf16[64,3,1024]{2,0,1:T(8,128)(2,1)} %bitcast.2) | data formatting | bytes 786432
